TPU v7x, 16 devices: a 4x2x1 block of a 4x4x8 slice. The times are simulated.
16 devices in a mesh: dp: 2 (over y, z), ep: 8 (over x, core).
Axes of the slice: x: 4, y: 2, z: 1, core: 2. Of those that a mesh axis runs over, the one named last changes fastest.
The devices are a block of a 4x4x8 slice.
Arguments:
- resid_in: bfloat16 [4096, 2560], P(('dp', 'ep')), parts along dimension 0
- expert_ids: int32 [4096, 6], P(('dp', 'ep')), parts along dimension 0
- priority: int32 [4096, 6], P(('dp', 'ep')), parts along dimension 0
- norm_gain: float32 [2560], replicated
- router_w: bfloat16 [2560, 64], replicated
- shared_w1: bfloat16 [2560, 3072], replicated
- shared_w3: bfloat16 [2560, 3072], replicated
- shared_w2: bfloat16 [3072, 2560], replicated
- expert_w1: bfloat16 [64, 2560, 1536], P('ep')
- expert_w3: bfloat16 [64, 2560, 1536], P('ep')
- expert_w2: bfloat16 [64, 1536, 2560], P('ep')
Outputs:
- output: bfloat16 [4096, 2560], P(('dp', 'ep')), parts along dimension 0
There are 2 independent parts. A program takes and returns all parts, laid end to end along the dimension named above; an argument that names none is the same for every part.
All inputs are finite; a program needn't handle non-finite values.
Results may differ from a plain program's by a relative error of at most 0.00678837.
Values are sent between devices in bfloat16 or wider.
A program may use at most 768 MiB of HBM per device.

v0:
```python
import functools
import jax
import jax.numpy as jnp
from jax import lax
from jax.experimental import pallas as pl
from jax.experimental.pallas import tpu as pltpu
from jax.sharding import PartitionSpec as P

NORM_EPS = 1e-6
ROUTE_SCALE = 16.0
LANES = 128
ROW_TILE = 256
ALIGN = 16
VMEM_LIMIT = 60 * 1024 * 1024
F32, BF16, I32 = jnp.float32, jnp.bfloat16, jnp.int32


def rms_norm(resid_in, norm_gain):
    resid32 = resid_in.astype(F32)
    inv_rms = lax.rsqrt(jnp.mean(resid32 * resid32, axis=1, keepdims=True) + NORM_EPS)
    return (resid32 * inv_rms * norm_gain).astype(BF16)


def gate_values(normed, router_w, expert_ids):
    probs = jax.nn.softmax(jnp.dot(normed, router_w, preferred_element_type=F32), axis=1)
    hit = expert_ids[:, :, None] == jnp.arange(probs.shape[1], dtype=I32)
    return ROUTE_SCALE * jnp.sum(jnp.where(hit, probs[:, None, :], 0.0), axis=2)


def dispatch(meta, normed, local_experts, capacity, slots, ep_size):
    meta_rows, tok_local = meta.shape
    width = normed.shape[1]
    chips = ep_size // 2
    n_tokens = ep_size * tok_local
    half = tok_local // 2
    chunks = 5
    piece = width // chunks
    halves = tok_local // LANES
    tok_tiles = ep_size * halves
    n_rows = tok_tiles * 8
    used = capacity + local_experts * ALIGN
    slot_tiles = used // LANES
    sel_step = used // 4
    moves = [(dc, ds) for ds in range(2) for dc in range(chips) if (dc, ds) != (0, 0)]
    seen_from = {0: 0, 1: 1, chips - 1: 2, 2: 3}

    def kernel(meta_ref, x_ref, out_ref, tok_ref, gate_ref, span_ref,
               meta_all, rows_all, sel, picked, pos_scr, gate_rows, aux_scr,
               meta_send, meta_recv, send_sem, recv_sem, out_sem):
        me = lax.axis_index('ep')
        chip, core = me // 2, lax.rem(me, 2)

        def peer(dc, ds):
            return 2 * lax.rem(chip + dc, chips) + (core if ds == 0 else 1 - core)

        sibling, after, before = peer(0, 1), peer(1, 0), peer(chips - 1, 0)

        def remote(src, dst, send, recv, device):
            return pltpu.make_async_remote_copy(src_ref=src, dst_ref=dst, send_sem=send, recv_sem=recv,
                                                device_id={'ep': device}, device_id_type=pl.DeviceIdType.MESH)

        barrier = pltpu.get_barrier_semaphore()
        for dc, ds in moves:
            pl.semaphore_signal(barrier, inc=1, device_id={'ep': peer(dc, ds)}, device_id_type=pl.DeviceIdType.MESH)
        pl.semaphore_wait(barrier, len(moves))

        meta_copies = [remote(meta_ref, meta_all.at[4 * ds + seen_from[dc]], meta_send.at[i], meta_recv.at[i], peer(dc, ds))
                       for i, (dc, ds) in enumerate(moves)]
        for copy in meta_copies:
            copy.start()

        def block(c, b, first=0, count=tok_local):
            return rows_all.at[c, pl.ds(b * tok_local + first, count), :]

        def move(kind, c):
            own = x_ref.at[:, pl.ds(c * piece, piece)]
            src, dst, device = [
                (own, block(c, 1), after),
                (own, block(c, 2), before),
                (own, block(c, 4), sibling),
                (block(c, 1, 0, half), block(c, 3, 0, half), after),
                (block(c, 2, half, half), block(c, 3, half, half), before),
                (block(c, 1), block(c, 5), sibling),
                (block(c, 2), block(c, 6), sibling),
                (block(c, 3, 0, half), block(c, 7, 0, half), sibling),
                (block(c, 3, half, half), block(c, 7, half, half), sibling)][kind]
            return remote(src, dst, send_sem.at[kind, c], recv_sem.at[kind, c], device)

        def send_own(c):
            for kind in (0, 1, 2):
                move(kind, c).start()

        def pass_on(c):
            move(0, c).wait_recv()
            move(3, c).start()
            move(5, c).start()
            move(1, c).wait_recv()
            move(4, c).start()
            move(6, c).start()

        def pass_opposite(c):
            move(3, c).wait_recv()
            move(7, c).start()
            move(4, c).wait_recv()
            move(8, c).start()

        def take_rest(c):
            for kind in (2, 5, 6, 7, 8):
                move(kind, c).wait_recv()

        send_own(0)
        send_own(1)
        meta_all[0] = meta_ref[...]
        for c in range(chunks):
            rows_all[c, 0:tok_local, :] = x_ref[:, c * piece:(c + 1) * piece]
        for copy in meta_copies:
            copy.wait_recv()

        def rows(first):
            return jnp.concatenate([meta_all[b, first:first + 8, h * LANES:(h + 1) * LANES] for b in range(ep_size) for h in range(halves)], axis=0)

        local_e = rows(0) - (me * local_experts).astype(F32)
        prio = rows(8)
        gates = rows(16)
        mine = (local_e >= 0.0) & (local_e < float(local_experts))
        mine_prio = jnp.where(mine, prio, 1.0e9)
        thresh = jnp.zeros((1, 1), F32)
        bit = 1
        while bit < n_rows * LANES:
            bit *= 2
        while bit >= 1:
            trial = thresh + float(bit)
            count = jnp.sum(jnp.where(mine_prio < trial, 1.0, 0.0), keepdims=True).reshape(1, 1)
            thresh = jnp.where(count <= float(capacity), trial, thresh)
            bit //= 2
        kept = mine & (prio < thresh)
        row_i = lax.broadcasted_iota(I32, (LANES, LANES), 0)
        col_i = lax.broadcasted_iota(I32, (LANES, LANES), 1)
        upper = jnp.where(row_i < col_i, 1.0, 0.0).astype(BF16)
        lower_r = lax.broadcasted_iota(I32, (n_rows, n_rows), 0)
        lower_c = lax.broadcasted_iota(I32, (n_rows, n_rows), 1)
        lower = jnp.where(lower_c < lower_r, 1.0, 0.0).astype(BF16)
        span_lane = lax.broadcasted_iota(I32, (1, LANES), 1)
        pos = jnp.full((n_rows, LANES), -1.0, F32)
        start = jnp.zeros((1, 1), F32)
        starts = []
        spans = jnp.zeros((1, LANES), F32)
        for e in range(local_experts):
            hit = kept & (local_e == float(e))
            ones = jnp.where(hit, 1.0, 0.0)
            ones16 = ones.astype(BF16)
            in_row = jnp.dot(ones16, upper, preferred_element_type=F32)
            above = jnp.sum(jnp.dot(lower, ones16, preferred_element_type=F32), axis=1, keepdims=True)
            pos = jnp.where(hit, start + in_row + above, pos)
            count = jnp.sum(ones, keepdims=True).reshape(1, 1)
            starts.append(start)
            spans = jnp.where(span_lane == e, start, spans)
            spans = jnp.where(span_lane == local_experts + e, count, spans)
            start = start + jnp.floor((count + float(ALIGN - 1)) * (1.0 / ALIGN)) * float(ALIGN)
            of_e = jnp.where(hit, gates, 0.0)
            for t in range(tok_tiles):
                gate_rows[e:e + 1, t * LANES:(t + 1) * LANES] = jnp.sum(of_e[t * 8:t * 8 + 8, :], axis=0, keepdims=True)
        pos_scr[...] = pos
        span_ref[...] = spans.astype(I32)

        def build(i, carry):
            s_id = (row_i + i * LANES).astype(F32)
            for t in range(tok_tiles):
                any_hit = None
                for k in range(6):
                    r = t * 8 + k
                    eq = pos_scr[r:r + 1, :] == s_id
                    any_hit = eq if any_hit is None else any_hit | eq
                sel[pl.ds(pl.multiple_of(i * LANES, LANES), LANES), t * LANES:(t + 1) * LANES] = jnp.where(any_hit, 1.0, 0.0).astype(BF16)
            return carry

        pass_on(0)
        send_own(2)
        third = slot_tiles // 3
        lax.fori_loop(0, third, build, 0)
        pass_on(1)
        send_own(3)
        lax.fori_loop(third, 2 * third, build, 0)
        pass_opposite(0)
        lax.fori_loop(2 * third, slot_tiles, build, 0)
        pass_on(2)
        send_own(4)

        g32 = gate_rows[...]
        g_hi = g32.astype(BF16)
        rest = g32 - g_hi.astype(F32)
        g_mid = rest.astype(BF16)
        g_lo = (rest - g_mid.astype(F32)).astype(BF16)
        tok_i = lax.broadcasted_iota(I32, (8, n_tokens), 1)
        kind_i = lax.broadcasted_iota(I32, (8, n_tokens), 0)
        numbers = jnp.where(kind_i == 0, tok_i // ALIGN, jnp.where(kind_i == 1, lax.rem(tok_i, ALIGN), 1)).astype(F32).astype(BF16)
        table = jnp.concatenate([g_hi.astype(F32), g_mid.astype(F32), g_lo.astype(F32), numbers.astype(F32)], axis=0).astype(BF16)
        aux_scr[...] = lax.dot_general(sel[...], table, (((1,), (1,)), ((), ())), preferred_element_type=F32)
        eye = row_i == col_i
        lane32 = lax.broadcasted_iota(I32, (LANES, 32), 1)
        sub32 = lax.broadcasted_iota(I32, (LANES, 32), 0)

        def table_row(i, carry):
            aux = aux_scr[pl.ds(pl.multiple_of(i * LANES, LANES), LANES), :]
            s_id = (sub32 + i * LANES).astype(F32)
            owner = jnp.zeros((LANES, 32), F32)
            for e in range(1, local_experts):
                owner = owner + jnp.where(s_id >= starts[e], 1.0, 0.0)
            is_gate = (lane32 < 24) & (lax.rem(lane32, 8).astype(F32) == owner)
            gate_col = jnp.sum(jnp.where(is_gate, aux, 0.0), axis=1, keepdims=True)
            tok_w = jnp.where(lane32 == 24, float(ALIGN), jnp.where(lane32 == 25, 1.0, 0.0))
            hit_col = jnp.sum(jnp.where(lane32 == 26, aux, 0.0), axis=1, keepdims=True)
            tok_col = jnp.sum(aux * tok_w, axis=1, keepdims=True)
            tok_col = jnp.where(hit_col > 0.5, tok_col, float(n_tokens))
            tok_ref[pl.ds(i, 1), :] = jnp.sum(jnp.where(eye, tok_col, 0.0), axis=0, keepdims=True).astype(I32)
            gate_ref[pl.ds(i, 1), :] = jnp.sum(jnp.where(eye, gate_col, 0.0), axis=0, keepdims=True)
            return carry

        lax.fori_loop(0, slot_tiles, table_row, 0)

        def out_copy(c):
            return pltpu.make_async_copy(picked.at[c % 2], out_ref.at[pl.ds(0, used), pl.ds(c * piece, piece)], out_sem.at[c % 2])

        def pick(c):
            take_rest(c)
            if c >= 2:
                out_copy(c - 2).wait()

            def step(i, carry):
                at = pl.ds(pl.multiple_of(i * sel_step, ALIGN), sel_step)
                picked[c % 2, at, :] = jnp.dot(sel[at, :], rows_all[c], preferred_element_type=F32).astype(BF16)
                return carry

            lax.fori_loop(0, used // sel_step, step, 0)
            out_copy(c).start()

        pass_opposite(1)
        pick(0)
        pass_on(3)
        pass_opposite(2)
        pick(1)
        pass_on(4)
        pass_opposite(3)
        pick(2)
        pass_opposite(4)
        pick(3)
        pick(4)
        out_copy(3).wait()
        out_copy(4).wait()
        for copy in meta_copies:
            copy.wait_send()
        for c in range(chunks):
            for kind in range(9):
                move(kind, c).wait_send()

    vmem = pl.BlockSpec(memory_space=pltpu.VMEM)
    dma = pltpu.SemaphoreType.DMA
    table_rows = -(-slot_tiles // 8) * 8
    return pl.pallas_call(
        kernel,
        out_shape=(
            jax.ShapeDtypeStruct((slots, width), BF16),
            jax.ShapeDtypeStruct((table_rows, LANES), I32),
            jax.ShapeDtypeStruct((table_rows, LANES), F32),
            jax.ShapeDtypeStruct((1, LANES), I32)),
        in_specs=[vmem, vmem],
        out_specs=(pl.BlockSpec(memory_space=pl.ANY), vmem, vmem, vmem),
        scratch_shapes=[
            pltpu.VMEM((ep_size, meta_rows, tok_local), F32), pltpu.VMEM((chunks, n_tokens, piece), BF16),
            pltpu.VMEM((used, n_tokens), BF16), pltpu.VMEM((2, used, piece), BF16),
            pltpu.VMEM((n_rows, LANES), F32), pltpu.VMEM((local_experts, n_tokens), F32), pltpu.VMEM((used, 32), F32),
            dma((len(moves),)), dma((len(moves),)), dma((9, chunks)), dma((9, chunks)), dma((2,))],
        compiler_params=pltpu.CompilerParams(collective_id=0, has_side_effects=True, vmem_limit_bytes=VMEM_LIMIT),
        name='dispatch',
    )(meta, normed)


def expert_hidden(spans, rows_in, expert_w1, expert_w3):
    slots, width = rows_in.shape
    local_experts, _, ff = expert_w1.shape
    block = ff // 2

    def kernel(span_ref, x_ref, w1_ref, w3_ref, h_ref):
        e = pl.program_id(0)
        n = pl.program_id(1)
        start = span_ref[e]
        count = span_ref[local_experts + e]
        col = pl.multiple_of(n * block, LANES)

        def tile(i, carry):
            at = pl.ds(pl.multiple_of(start + i * ROW_TILE, ALIGN), ROW_TILE)
            x = x_ref[at, :]
            up_a = jnp.dot(x, w1_ref[0], preferred_element_type=F32)
            up_b = jnp.dot(x, w3_ref[0], preferred_element_type=F32)
            h_ref[at, pl.ds(col, block)] = (jax.nn.silu(up_a) * up_b).astype(BF16)
            return carry

        lax.fori_loop(0, (count + ROW_TILE - 1) // ROW_TILE, tile, 0)

    w_spec = pl.BlockSpec((1, width, block), lambda e, n, span: (e, 0, n))
    return pl.pallas_call(
        kernel,
        out_shape=jax.ShapeDtypeStruct((slots, ff), BF16),
        grid_spec=pltpu.PrefetchScalarGridSpec(
            num_scalar_prefetch=1, grid=(local_experts, ff // block),
            in_specs=[pl.BlockSpec((slots, width), lambda e, n, span: (0, 0)), w_spec, w_spec],
            out_specs=pl.BlockSpec((slots, ff), lambda e, n, span: (0, 0))),
        compiler_params=pltpu.CompilerParams(vmem_limit_bytes=VMEM_LIMIT, dimension_semantics=('arbitrary', 'arbitrary')),
        cost_estimate=pl.CostEstimate(flops=4 * 1536 * width * ff, bytes_accessed=2 * expert_w1.size * 2, transcendentals=slots * ff),
        name='expert_hidden',
    )(spans, rows_in, expert_w1, expert_w3)


def expert_combine(spans, slot_tok, slot_gate, hidden, expert_w2, n_tokens):
    slots, ff = hidden.shape
    local_experts, _, width = expert_w2.shape
    cols = width // 2
    groups = cols // LANES
    batch = 8

    def kernel(span_ref, tok_ref, gate_ref, h_ref, w2_ref, acc_ref, row_scr):
        e = pl.program_id(1)

        @pl.when(e == 0)
        def _():
            acc_ref[...] = jnp.zeros_like(acc_ref)

        start = span_ref[e]
        count = span_ref[local_experts + e]

        def tile(i, carry):
            base = start + i * ROW_TILE
            h = h_ref[pl.ds(pl.multiple_of(base, ALIGN), ROW_TILE), :]
            out = jnp.dot(h, w2_ref[0], preferred_element_type=F32).astype(BF16).astype(F32)
            for g in range(groups):
                row_scr[pl.ds(g, ROW_TILE, stride=groups), :] = out[:, g * LANES:(g + 1) * LANES]

            def add_rows(q, inner):
                ats, new = [], []
                for u in range(batch):
                    s = base + q * batch + u
                    at = pl.ds(tok_ref[s] * groups, groups)
                    ats.append(at)
                    new.append(acc_ref[0, at, :] + gate_ref[s] * row_scr[pl.ds((q * batch + u) * groups, groups), :])
                for at, value in zip(ats, new):
                    acc_ref[0, at, :] = value
                return inner

            todo = jnp.minimum(count - i * ROW_TILE, ROW_TILE)
            lax.fori_loop(0, (todo + batch - 1) // batch, add_rows, 0)
            return carry

        lax.fori_loop(0, (count + ROW_TILE - 1) // ROW_TILE, tile, 0)

    acc_rows = (n_tokens + 8) * groups
    return pl.pallas_call(
        kernel,
        out_shape=jax.ShapeDtypeStruct((2, acc_rows, LANES), F32),
        grid_spec=pltpu.PrefetchScalarGridSpec(
            num_scalar_prefetch=3, grid=(2, local_experts),
            in_specs=[pl.BlockSpec((slots, ff), lambda n, e, *_: (0, 0)),
                      pl.BlockSpec((1, ff, cols), lambda n, e, *_: (e, 0, n))],
            out_specs=pl.BlockSpec((1, acc_rows, LANES), lambda n, e, *_: (n, 0, 0)),
            scratch_shapes=[pltpu.VMEM((ROW_TILE * groups, LANES), F32)]),
        compiler_params=pltpu.CompilerParams(vmem_limit_bytes=VMEM_LIMIT, dimension_semantics=('arbitrary', 'arbitrary')),
        cost_estimate=pl.CostEstimate(flops=2 * 1536 * ff * width, bytes_accessed=expert_w2.size * 2, transcendentals=0),
        name='expert_combine',
    )(spans, slot_tok, slot_gate, hidden, expert_w2)


def reduce_and_finish(sums, resid_in, normed, shared_w1, shared_w3, shared_w2, ep_size):
    chips = ep_size // 2
    tok_local, width = resid_in.shape
    ff = shared_w1.shape[1]
    groups = width // 2 // LANES
    pieces = 4
    tok_piece = tok_local // 2
    piece_rows = tok_piece * groups
    up_cols = 512
    n_up = ff // up_cols
    down_cols = 512
    n_down = width // down_cols
    add_step = 128

    def kernel(sums_ref, resid_ref, x_ref, w1_ref, w3_ref, w2_ref, out_ref,
               own, pair, opp, home, up_buf, down_buf, hid, shared,
               load_sem, pair_send, pair_recv, fwd_send, fwd_recv, bwd_send, bwd_recv, up_sem, down_sem):
        me = lax.axis_index('ep')
        chip, core = me // 2, lax.rem(me, 2)
        sibling = 2 * chip + 1 - core
        after = 2 * lax.rem(chip + 1, chips) + core
        before = 2 * lax.rem(chip + chips - 1, chips) + core

        def up_copy(j, slot, which):
            src = w1_ref if which == 0 else w3_ref
            return pltpu.make_async_copy(src.at[:, pl.ds(pl.multiple_of(j * up_cols, LANES), up_cols)], up_buf.at[slot, which], up_sem.at[slot, which])

        def down_copy(j, slot):
            return pltpu.make_async_copy(w2_ref.at[:, pl.ds(pl.multiple_of(j * down_cols, LANES), down_cols)], down_buf.at[slot], down_sem.at[slot])

        barrier = pltpu.get_barrier_semaphore()
        for peer in (sibling, after, before):
            pl.semaphore_signal(barrier, inc=1, device_id={'ep': peer}, device_id_type=pl.DeviceIdType.MESH)
        pl.semaphore_wait(barrier, 3)

        def block_piece(b, q):
            return sums_ref.at[q // 2, pl.ds((b * 2 + q % 2) * piece_rows, piece_rows), :]

        def load(o, q):
            return pltpu.make_async_copy(block_piece(o, q), own.at[o, q], load_sem.at[o, q])

        def to_pair(o, q):
            return pltpu.make_async_remote_copy(
                src_ref=block_piece(chips + o, q), dst_ref=pair.at[o, q], send_sem=pair_send.at[o, q], recv_sem=pair_recv.at[o, q],
                device_id={'ep': sibling}, device_id_type=pl.DeviceIdType.MESH)

        def ring(src, dst, send, recv, i, peer):
            return pltpu.make_async_remote_copy(
                src_ref=src, dst_ref=dst, send_sem=send.at[i], recv_sem=recv.at[i],
                device_id={'ep': peer}, device_id_type=pl.DeviceIdType.MESH)

        order = [(o, q) for o in (3, 2, 1, 0) for q in ((0, 2, 1, 3) if o == 3 else (2, 3, 0, 1) if o == 2 else (0, 1, 2, 3))]
        for o, q in order:
            to_pair(o, q).start()
            load(o, q).start()
        for slot in range(2):
            for which in range(2):
                up_copy(slot, slot, which).start()

        def add(o, q, src):
            def step(i, carry):
                at = pl.ds(pl.multiple_of(i * add_step, add_step), add_step)
                own[o, q, at, :] = own[o, q, at, :] + src[at, :]
                return carry

            lax.fori_loop(0, piece_rows // add_step, step, 0)

        def pair_sum(o, q):
            load(o, q).wait()
            to_pair(o, q).wait_recv()
            add(o, q, pair.at[o, q])

        opp_fwd = [ring(own.at[3, q], opp.at[q], fwd_send, fwd_recv, q, after) for q in (0, 1)]
        opp_bwd = [ring(own.at[3, 2 + q], opp.at[2 + q], bwd_send, bwd_recv, q, before) for q in (0, 1)]
        home_fwd = {q: ring(own.at[2, q], home.at[0, q], fwd_send, fwd_recv, 2 + q, after) for q in range(pieces)}
        home_bwd = {q: ring(own.at[1, q], home.at[1, q], bwd_send, bwd_recv, 2 + q, before) for q in range(pieces)}
        for q in (0, 1):
            pair_sum(3, q)
            pair_sum(3, 2 + q)
            opp_fwd[q].start()
            opp_bwd[q].start()
        for q in (0, 1):
            pair_sum(2, 2 + q)
            pair_sum(1, q)
            home_fwd[2 + q].start()
            home_bwd[q].start()
        for q in (0, 1):
            pair_sum(2, q)
            pair_sum(1, 2 + q)

        def up_step(j, carry):
            slot = lax.rem(j, 2)
            up_copy(j, slot, 0).wait()
            up_copy(j, slot, 1).wait()
            up_a = jnp.dot(x_ref[...], up_buf[slot, 0], preferred_element_type=F32)
            up_b = jnp.dot(x_ref[...], up_buf[slot, 1], preferred_element_type=F32)
            hid[:, pl.ds(pl.multiple_of(j * up_cols, LANES), up_cols)] = (jax.nn.silu(up_a) * up_b).astype(BF16)

            @pl.when(j + 2 < n_up)
            def _():
                up_copy(j + 2, slot, 0).start()
                up_copy(j + 2, slot, 1).start()

            return carry

        for slot in range(2):
            down_copy(slot, slot).start()
        lax.fori_loop(0, n_up, up_step, 0)

        def down_step(j, carry):
            slot = lax.rem(j, 2)
            down_copy(j, slot).wait()
            part = jnp.dot(hid[...], down_buf[slot], preferred_element_type=F32)
            shared[:, pl.ds(pl.multiple_of(j * down_cols, LANES), down_cols)] = part.astype(BF16)

            @pl.when(j + 2 < n_down)
            def _():
                down_copy(j + 2, slot).start()

            return carry

        lax.fori_loop(0, n_down, down_step, 0)

        for q in range(pieces):
            pair_sum(0, q)
        for q in (0, 1):
            opp_fwd[q].wait_recv()
            add(2, q, opp.at[q])
            home_fwd[q].start()
            opp_bwd[q].wait_recv()
            add(1, 2 + q, opp.at[2 + q])
            home_bwd[2 + q].start()
        for q in (0, 2, 1, 3):
            home_fwd[q].wait_recv()
            home_bwd[q].wait_recv()
            add(0, q, home.at[0, q])
            add(0, q, home.at[1, q])
            rows = slice((q % 2) * tok_piece, (q % 2 + 1) * tok_piece)
            for g in range(groups):
                col = (q // 2 * groups + g) * LANES
                routed = own[0, q, pl.ds(g, tok_piece, stride=groups), :]
                total = resid_ref[rows, col:col + LANES].astype(F32) + shared[rows, col:col + LANES].astype(F32) + routed
                out_ref[rows, col:col + LANES] = total.astype(BF16)
        for o, q in order:
            to_pair(o, q).wait_send()
        for copy in opp_fwd + opp_bwd + list(home_fwd.values()) + list(home_bwd.values()):
            copy.wait_send()

    hbm = pl.BlockSpec(memory_space=pl.ANY)
    vmem = pl.BlockSpec(memory_space=pltpu.VMEM)
    dma = pltpu.SemaphoreType.DMA
    return pl.pallas_call(
        kernel,
        out_shape=jax.ShapeDtypeStruct((tok_local, width), BF16),
        in_specs=[hbm, vmem, vmem, hbm, hbm, hbm],
        out_specs=vmem,
        scratch_shapes=[
            pltpu.VMEM((chips, pieces, piece_rows, LANES), F32), pltpu.VMEM((chips, pieces, piece_rows, LANES), F32),
            pltpu.VMEM((pieces, piece_rows, LANES), F32), pltpu.VMEM((2, pieces, piece_rows, LANES), F32),
            pltpu.VMEM((2, 2, width, up_cols), BF16), pltpu.VMEM((2, ff, down_cols), BF16),
            pltpu.VMEM((tok_local, ff), BF16), pltpu.VMEM((tok_local, width), BF16),
            dma((chips, pieces)), dma((chips, pieces)), dma((chips, pieces)), dma((6,)), dma((6,)), dma((6,)), dma((6,)), dma((2, 2)), dma((2,))],
        compiler_params=pltpu.CompilerParams(collective_id=1, has_side_effects=True, vmem_limit_bytes=VMEM_LIMIT),
        cost_estimate=pl.CostEstimate(flops=6 * tok_local * width * ff, bytes_accessed=6 * width * ff, transcendentals=tok_local * ff),
        name='reduce_and_finish',
    )(sums, resid_in, normed, shared_w1, shared_w3, shared_w2)


def solution(mesh):
    ep_size = mesh.shape['ep']
    tok_spec = P(('dp', 'ep'))
    expert_spec = P('ep')

    def device_fn(resid_in, expert_ids, priority, norm_gain, router_w, shared_w1, shared_w3, shared_w2, expert_w1, expert_w3, expert_w2):
        tok_local, width = resid_in.shape
        top_k = expert_ids.shape[1]
        local_experts = expert_w1.shape[0]
        capacity = tok_local * top_k
        n_tokens = tok_local * ep_size
        slots = -(-(capacity + local_experts * ALIGN + ROW_TILE) // LANES) * LANES
        normed = rms_norm(resid_in, norm_gain)
        gates = gate_values(normed, router_w, expert_ids)

        def rows8(x, fill):
            return jnp.pad(x.astype(F32).T, ((0, 8 - top_k), (0, 0)), constant_values=fill)

        meta = jnp.concatenate([rows8(expert_ids, -1.0e6), rows8(priority, 0.0), rows8(gates, 0.0)], axis=0)
        rows_in, slot_tok, slot_gate, spans = dispatch(meta, normed, local_experts, capacity, slots, ep_size)
        spans = spans.reshape(-1)
        hidden = expert_hidden(spans, rows_in, expert_w1, expert_w3)
        sums = expert_combine(spans, slot_tok.reshape(-1), slot_gate.reshape(-1), hidden, expert_w2, n_tokens)
        return reduce_and_finish(sums, resid_in, normed, shared_w1, shared_w3, shared_w2, ep_size)

    return jax.shard_map(device_fn, mesh=mesh, in_specs=(tok_spec, tok_spec, tok_spec, P(), P(), P(), P(), P(), expert_spec, expert_spec, expert_spec), out_specs=tok_spec, check_vma=False)
```

profile of v0, /device:TPU:113, one launch (start us, length us, event | category | flops | bytes accessed | tf_op | source)
XLA Modules:
  0.0 264.0 jit_solution(13498734061519455519)
XLA Ops:
  0.0 0.0 copy-start
  0.0 0.0 copy-start.3
  0.0 1.7 fusion
  1.7 0.7 convert_bitcast_fusion
  2.4 1.7 fusion.2.x_ref
  4.1 0.0 copy-done
  4.1 0.0 copy-start.2
  4.1 0.5 fusion.6
  4.7 0.0 copy-done.3
  4.8 0.1 select_reduce_fusion
  4.8 0.6 select_maximum_fusion.meta_ref
  5.5 0.0 copy-done.2
  5.5 64.0 %dispatch.1 = (bf16[1920,2560]{1,0:T(8,128)(2,1)}, s32[16,128]{1,0:T(8,128)}, f32[16,128]{1,0:T(8,128)}, s32[1,128]{1,0:T(1,128)}) custom-call(f32[24,256]{1,0:T(8,128)} %select_maximum_fusion.meta_ref, bf16[256,2560]{1,0:T(8,128)(2,1)} %copy-done.2), custom_call_target="tpu_custom_call" | custom-call | tf_op jit(solution)/shard_map/dispatch/pallas_call | solution.py:259
  69.4 53.2 %expert_hidden.1.h_ref = bf16[1920,1536]{1,0:T(8,128)(2,1)} custom-call(s32[128]{0:T(128)} %bitcast.13, bf16[1920,2560]{1,0:T(8,128)(2,1)} %get-tuple-element.12.x_ref, bf16[8,2560,1536]{2,1,0:T(8,128)(2,1)} %w1_ref.2, bf16[8,2560,1536]{2,1,0:T(8,128)(2,1)} %w3_ref.2), custom_call_target="tpu_custom_call" | custom-call | flops 24159191040 | bytes 125829120 | tf_op jit(solution)/shard_map/expert_hidden/pallas_call | solution.py:301
  122.6 43.1 %expert_combine.1.sums_ref = f32[2,20560,128]{2,1,0:T(8,128)} custom-call(s32[128]{0:T(128)} %bitcast.14, s32[2048]{0:T(1024)} %bitcast.11, f32[2048]{0:T(1024)} %bitcast.12, bf16[1920,1536]{1,0:T(8,128)(2,1)} %expert_hidden.1.h_ref, bf16[8,1536,2560]{2,1,0:T(8,128)(2,1)} %w2_ref.2), custom_call_target="tpu_custom_call" | custom-call | flops 12079595520 | bytes 62914560 | tf_op jit(solution)/shard_map/expert_combine/pallas_call | solution.py:356
  165.7 0.0 copy-start.1
  165.8 95.8 %reduce_and_finish.1 = bf16[256,2560]{1,0:T(8,128)(2,1)} custom-call(f32[2,20560,128]{2,1,0:T(8,128)} %expert_combine.1.sums_ref, bf16[256,2560]{1,0:T(8,128)(2,1)} %resid_ref.1, bf16[256,2560]{1,0:T(8,128)(2,1)} %copy-done.2, bf16[2560,3072]{1,0:T(8,128)(2,1)} %w1_ref.3, bf16[2560,3072]{1,0:T(8,128)(2,1)} %w3_ref.3, bf16[3072,2560]{1,0:T(8,128)(2,1)} %w2_ref.3), custom_call_target="tpu_custom_call" | custom-call | flops 12079595520 | bytes 47185920 | tf_op jit(solution)/shard_map/reduce_and_finish/pallas_call | solution.py:522
  261.6 2.5 copy.15
  264.0 0.0 copy-done.1
  (4 shorter events, 0.1 us)
Async XLA Ops:
  0.0 4.1 %copy-start = (bf16[2560,64]{0,1:T(8,128)(2,1)S(1)}, bf16[2560,64]{0,1:T(8,128)(2,1)}, u32[]{:S(2)}) copy-start(bf16[2560,64]{0,1:T(8,128)(2,1)} %param.15) | copy-start | bytes 983044
  0.0 4.7 %copy-start.3 = (s32[256,6]{0,1:T(8,128)S(1)}, s32[256,6]{0,1:T(8,128)}, u32[]{:S(2)}) copy-start(s32[256,6]{0,1:T(8,128)} %param.12) | copy-start | bytes 18436
  4.1 1.3 copy-start.2
  165.7 98.3 %copy-start.1 = (bf16[2560,64]{0,1:T(8,128)(2,1)S(1)}, bf16[2560,64]{0,1:T(8,128)(2,1)}, u32[]{:S(2)}) copy-start(bf16[2560,64]{0,1:T(8,128)(2,1)} %param.15) | copy-start | bytes 983044
where the time goes:
time: 265 us; the launch traced here: 264 us
  Pallas kernels  256 us (97%)
  other arithmetic  4.85 us (2%)
    pallas_call x1, Pallas kernels, reduce_and_finish(): pl.pallas_call(kernel, out_shape=jax.ShapeDtypeStruct((tok_local, width),...  95.8 us
    pallas_call x1, Pallas kernels, dispatch(): pl.pallas_call(kernel, out_shape=(jax.ShapeDtypeStruct((slots, width), BF...  64 us
    pallas_call x1, Pallas kernels, expert_hidden(): pl.pallas_call(kernel, out_shape=jax.ShapeDtypeStruct((slots, ff), BF16),...  53.2 us
    pallas_call x1, Pallas kernels, expert_combine(): pl.pallas_call(kernel, out_shape=jax.ShapeDtypeStruct((2, acc_rows, LANES...  43.1 us

commit v1 on v0

--- a/solution.py
+++ b/solution.py
@@ -275,65 +275,105 @@
     )(meta, normed)
 
 
-def expert_hidden(spans, rows_in, expert_w1, expert_w3):
+def experts(spans, slot_tok, slot_gate, rows_in, expert_w1, expert_w3, expert_w2, n_tokens, capacity):
     slots, width = rows_in.shape
     local_experts, _, ff = expert_w1.shape
-    block = ff // 2
-
-    def kernel(span_ref, x_ref, w1_ref, w3_ref, h_ref):
-        e = pl.program_id(0)
-        n = pl.program_id(1)
-        start = span_ref[e]
-        count = span_ref[local_experts + e]
-        col = pl.multiple_of(n * block, LANES)
-
-        def tile(i, carry):
-            at = pl.ds(pl.multiple_of(start + i * ROW_TILE, ALIGN), ROW_TILE)
-            x = x_ref[at, :]
-            up_a = jnp.dot(x, w1_ref[0], preferred_element_type=F32)
-            up_b = jnp.dot(x, w3_ref[0], preferred_element_type=F32)
-            h_ref[at, pl.ds(col, block)] = (jax.nn.silu(up_a) * up_b).astype(BF16)
+    groups = width // LANES
+    up_cols, n_up = 512, ff // 512
+    down_cols, n_down = width // 2, 2
+    down_groups = down_cols // LANES
+    max_items = local_experts + -(-capacity // ROW_TILE)
+    acc_rows = (n_tokens + 8) * groups
+    sizes = (128, 160, 192, 224, 256)
+    batch = 8
+
+    def kernel(span_ref, tok_ref, gate_ref, x_ref, w1_ref, w3_ref, w2_ref, out_ref,
+               acc, row_scr, hid, x_tile, up, down, item_e, item_base, item_count, x_sem, up_sem, down_sem, out_sem):
+        def plan(e, n):
+            count = span_ref[local_experts + e]
+
+            def one(j, m):
+                item_e[m] = e
+                item_base[m] = span_ref[e] + j * ROW_TILE
+                item_count[m] = jnp.minimum(count - j * ROW_TILE, ROW_TILE)
+                return m + 1
+
+            return lax.fori_loop(0, (count + ROW_TILE - 1) // ROW_TILE, one, n)
+
+        n_items = lax.fori_loop(0, local_experts, plan, 0)
+
+        def x_copy(i, slot):
+            return pltpu.make_async_copy(x_ref.at[pl.ds(pl.multiple_of(item_base[i], ALIGN), ROW_TILE), :], x_tile.at[slot], x_sem.at[slot])
+
+        def up_copy(i, k, which):
+            src = w1_ref if which == 0 else w3_ref
+            return pltpu.make_async_copy(src.at[item_e[i], :, pl.ds(k * up_cols, up_cols)], up.at[k, which], up_sem.at[k, which])
+
+        def down_copy(i, k):
+            return pltpu.make_async_copy(w2_ref.at[item_e[i], :, pl.ds(k * down_cols, down_cols)], down.at[k], down_sem.at[k])
+
+        @pl.when(n_items > 0)
+        def _():
+            x_copy(0, 0).start()
+            for k in range(n_up):
+                up_copy(0, k, 0).start()
+                up_copy(0, k, 1).start()
+            for k in range(n_down):
+                down_copy(0, k).start()
+
+        def zero(i, carry):
+            acc[pl.ds(pl.multiple_of(i * groups * 8, 8), groups * 8), :] = jnp.zeros((groups * 8, LANES), F32)
             return carry
 
-        lax.fori_loop(0, (count + ROW_TILE - 1) // ROW_TILE, tile, 0)
-
-    w_spec = pl.BlockSpec((1, width, block), lambda e, n, span: (e, 0, n))
-    return pl.pallas_call(
-        kernel,
-        out_shape=jax.ShapeDtypeStruct((slots, ff), BF16),
-        grid_spec=pltpu.PrefetchScalarGridSpec(
-            num_scalar_prefetch=1, grid=(local_experts, ff // block),
-            in_specs=[pl.BlockSpec((slots, width), lambda e, n, span: (0, 0)), w_spec, w_spec],
-            out_specs=pl.BlockSpec((slots, ff), lambda e, n, span: (0, 0))),
-        compiler_params=pltpu.CompilerParams(vmem_limit_bytes=VMEM_LIMIT, dimension_semantics=('arbitrary', 'arbitrary')),
-        cost_estimate=pl.CostEstimate(flops=4 * 1536 * width * ff, bytes_accessed=2 * expert_w1.size * 2, transcendentals=slots * ff),
-        name='expert_hidden',
-    )(spans, rows_in, expert_w1, expert_w3)
-
-
-def expert_combine(spans, slot_tok, slot_gate, hidden, expert_w2, n_tokens):
-    slots, ff = hidden.shape
-    local_experts, _, width = expert_w2.shape
-    cols = width // 2
-    groups = cols // LANES
-    batch = 8
-
-    def kernel(span_ref, tok_ref, gate_ref, h_ref, w2_ref, acc_ref, row_scr):
-        e = pl.program_id(1)
-
-        @pl.when(e == 0)
-        def _():
-            acc_ref[...] = jnp.zeros_like(acc_ref)
-
-        start = span_ref[e]
-        count = span_ref[local_experts + e]
-
-        def tile(i, carry):
-            base = start + i * ROW_TILE
-            h = h_ref[pl.ds(pl.multiple_of(base, ALIGN), ROW_TILE), :]
-            out = jnp.dot(h, w2_ref[0], preferred_element_type=F32).astype(BF16).astype(F32)
-            for g in range(groups):
-                row_scr[pl.ds(g, ROW_TILE, stride=groups), :] = out[:, g * LANES:(g + 1) * LANES]
+        lax.fori_loop(0, acc_rows // (groups * 8), zero, 0)
+
+        def item(i, carry):
+            slot = lax.rem(i, 2)
+            base = item_base[i]
+            count = item_count[i]
+            more = i + 1 < n_items
+            x_copy(i, slot).wait()
+
+            @pl.when(more)
+            def _():
+                x_copy(i + 1, 1 - slot).start()
+
+            def sized(body):
+                low = 0
+                for size in sizes:
+                    pl.when((count > low) & (count <= size))(functools.partial(body, size))
+                    low = size
+
+            for k in range(n_up):
+                up_copy(i, k, 0).wait()
+                up_copy(i, k, 1).wait()
+
+                def up_part(size, k=k):
+                    x = x_tile[slot, :size, :]
+                    up_a = jnp.dot(x, up[k, 0], preferred_element_type=F32)
+                    up_b = jnp.dot(x, up[k, 1], preferred_element_type=F32)
+                    hid[:size, k * up_cols:(k + 1) * up_cols] = (jax.nn.silu(up_a) * up_b).astype(BF16)
+
+                sized(up_part)
+
+                @pl.when(more)
+                def _(k=k):
+                    up_copy(i + 1, k, 0).start()
+                    up_copy(i + 1, k, 1).start()
+
+            for k in range(n_down):
+                down_copy(i, k).wait()
+
+                def down_part(size, k=k):
+                    out = jnp.dot(hid[:size, :], down[k], preferred_element_type=F32).astype(BF16).astype(F32)
+                    for g in range(down_groups):
+                        row_scr[pl.ds(k * down_groups + g, size, stride=groups), :] = out[:, g * LANES:(g + 1) * LANES]
+
+                sized(down_part)
+
+                @pl.when(more)
+                def _(k=k):
+                    down_copy(i + 1, k).start()
 
             def add_rows(q, inner):
                 ats, new = [], []
@@ -341,40 +381,45 @@
                     s = base + q * batch + u
                     at = pl.ds(tok_ref[s] * groups, groups)
                     ats.append(at)
-                    new.append(acc_ref[0, at, :] + gate_ref[s] * row_scr[pl.ds((q * batch + u) * groups, groups), :])
+                    new.append(acc[at, :] + gate_ref[s] * row_scr[pl.ds((q * batch + u) * groups, groups), :])
                 for at, value in zip(ats, new):
-                    acc_ref[0, at, :] = value
+                    acc[at, :] = value
                 return inner
 
-            todo = jnp.minimum(count - i * ROW_TILE, ROW_TILE)
-            lax.fori_loop(0, (todo + batch - 1) // batch, add_rows, 0)
+            lax.fori_loop(0, (count + batch - 1) // batch, add_rows, 0)
             return carry
 
-        lax.fori_loop(0, (count + ROW_TILE - 1) // ROW_TILE, tile, 0)
-
-    acc_rows = (n_tokens + 8) * groups
+        lax.fori_loop(0, n_items, item, 0)
+        out = pltpu.make_async_copy(acc, out_ref, out_sem)
+        out.start()
+        out.wait()
+
+    hbm = pl.BlockSpec(memory_space=pl.ANY)
+    dma = pltpu.SemaphoreType.DMA
     return pl.pallas_call(
         kernel,
-        out_shape=jax.ShapeDtypeStruct((2, acc_rows, LANES), F32),
+        out_shape=jax.ShapeDtypeStruct((acc_rows, LANES), F32),
         grid_spec=pltpu.PrefetchScalarGridSpec(
-            num_scalar_prefetch=3, grid=(2, local_experts),
-            in_specs=[pl.BlockSpec((slots, ff), lambda n, e, *_: (0, 0)),
-                      pl.BlockSpec((1, ff, cols), lambda n, e, *_: (e, 0, n))],
-            out_specs=pl.BlockSpec((1, acc_rows, LANES), lambda n, e, *_: (n, 0, 0)),
-            scratch_shapes=[pltpu.VMEM((ROW_TILE * groups, LANES), F32)]),
-        compiler_params=pltpu.CompilerParams(vmem_limit_bytes=VMEM_LIMIT, dimension_semantics=('arbitrary', 'arbitrary')),
-        cost_estimate=pl.CostEstimate(flops=2 * 1536 * ff * width, bytes_accessed=expert_w2.size * 2, transcendentals=0),
-        name='expert_combine',
-    )(spans, slot_tok, slot_gate, hidden, expert_w2)
+            num_scalar_prefetch=3, grid=(1,), in_specs=[hbm] * 4, out_specs=hbm,
+            scratch_shapes=[
+                pltpu.VMEM((acc_rows, LANES), F32), pltpu.VMEM((ROW_TILE * groups, LANES), F32),
+                pltpu.VMEM((ROW_TILE, ff), BF16), pltpu.VMEM((2, ROW_TILE, width), BF16),
+                pltpu.VMEM((n_up, 2, width, up_cols), BF16), pltpu.VMEM((n_down, ff, down_cols), BF16),
+                pltpu.SMEM((max_items,), I32), pltpu.SMEM((max_items,), I32), pltpu.SMEM((max_items,), I32),
+                dma((2,)), dma((n_up, 2)), dma((n_down,)), dma]),
+        compiler_params=pltpu.CompilerParams(vmem_limit_bytes=VMEM_LIMIT),
+        cost_estimate=pl.CostEstimate(flops=6 * capacity * width * ff, bytes_accessed=6 * local_experts * width * ff, transcendentals=capacity * ff),
+        name='experts',
+    )(spans, slot_tok, slot_gate, rows_in, expert_w1, expert_w3, expert_w2)
 
 
 def reduce_and_finish(sums, resid_in, normed, shared_w1, shared_w3, shared_w2, ep_size):
     chips = ep_size // 2
     tok_local, width = resid_in.shape
     ff = shared_w1.shape[1]
-    groups = width // 2 // LANES
+    groups = width // LANES
     pieces = 4
-    tok_piece = tok_local // 2
+    tok_piece = tok_local // pieces
     piece_rows = tok_piece * groups
     up_cols = 512
     n_up = ff // up_cols
@@ -404,7 +449,7 @@
         pl.semaphore_wait(barrier, 3)
 
         def block_piece(b, q):
-            return sums_ref.at[q // 2, pl.ds((b * 2 + q % 2) * piece_rows, piece_rows), :]
+            return sums_ref.at[pl.ds((b * pieces + q) * piece_rows, piece_rows), :]
 
         def load(o, q):
             return pltpu.make_async_copy(block_piece(o, q), own.at[o, q], load_sem.at[o, q])
@@ -505,9 +550,9 @@
             home_bwd[q].wait_recv()
             add(0, q, home.at[0, q])
             add(0, q, home.at[1, q])
-            rows = slice((q % 2) * tok_piece, (q % 2 + 1) * tok_piece)
+            rows = slice(q * tok_piece, (q + 1) * tok_piece)
             for g in range(groups):
-                col = (q // 2 * groups + g) * LANES
+                col = g * LANES
                 routed = own[0, q, pl.ds(g, tok_piece, stride=groups), :]
                 total = resid_ref[rows, col:col + LANES].astype(F32) + shared[rows, col:col + LANES].astype(F32) + routed
                 out_ref[rows, col:col + LANES] = total.astype(BF16)
@@ -557,8 +602,7 @@
         meta = jnp.concatenate([rows8(expert_ids, -1.0e6), rows8(priority, 0.0), rows8(gates, 0.0)], axis=0)
         rows_in, slot_tok, slot_gate, spans = dispatch(meta, normed, local_experts, capacity, slots, ep_size)
         spans = spans.reshape(-1)
-        hidden = expert_hidden(spans, rows_in, expert_w1, expert_w3)
-        sums = expert_combine(spans, slot_tok.reshape(-1), slot_gate.reshape(-1), hidden, expert_w2, n_tokens)
+        sums = experts(spans, slot_tok.reshape(-1), slot_gate.reshape(-1), rows_in, expert_w1, expert_w3, expert_w2, n_tokens, capacity)
         return reduce_and_finish(sums, resid_in, normed, shared_w1, shared_w3, shared_w2, ep_size)
 
     return jax.shard_map(device_fn, mesh=mesh, in_specs=(tok_spec, tok_spec, tok_spec, P(), P(), P(), P(), P(), expert_spec, expert_spec, expert_spec), out_specs=tok_spec, check_vma=False)

time: 265 us -> 238 us (0.90)
  Pallas kernels: 256 us -> 229 us
    pallas_call x2 -> x1, Pallas kernels: 96.3 us -> 68.5 us  [experts(): pl.pallas_call(kernel, out_shape=jax.ShapeDtypeStruct((acc_rows, LANES),...]
where the time goes in v1:
time: 238 us; the launch traced here: 237 us
  Pallas kernels  229 us (96%)
  other arithmetic  4.83 us (2%)
  local copies, waits for them, and re-layouts  2.48 us (1%)
    pallas_call x1, Pallas kernels, reduce_and_finish(): pl.pallas_call(kernel, out_shape=jax.ShapeDtypeStruct((tok_local, width),...  96.7 us
    pallas_call x1, Pallas kernels, experts(): pl.pallas_call(kernel, out_shape=jax.ShapeDtypeStruct((acc_rows, LANES),...  68.5 us
    pallas_call x1, Pallas kernels, dispatch(): pl.pallas_call(kernel, out_shape=(jax.ShapeDtypeStruct((slots, width), BF...  64 us

profile of v1, /device:TPU:113, one launch (start us, length us, event | category | flops | bytes accessed | tf_op | source)
XLA Modules:
  0.0 237.1 jit_solution(15246291592919168423)
XLA Ops:
  0.0 0.0 copy-start
  0.0 0.0 copy-start.3
  0.0 1.7 fusion
  1.7 0.7 convert_bitcast_fusion
  2.4 1.7 fusion.2.x_ref
  4.1 0.0 copy-done
  4.1 0.0 copy-start.2
  4.1 0.5 fusion.6
  4.7 0.0 copy-done.3
  4.8 0.1 select_reduce_fusion
  4.8 0.6 select_maximum_fusion.meta_ref
  5.4 0.0 copy-done.2
  5.4 64.0 %dispatch.1 = (bf16[1920,2560]{1,0:T(8,128)(2,1)}, s32[16,128]{1,0:T(8,128)}, f32[16,128]{1,0:T(8,128)}, s32[1,128]{1,0:T(1,128)}) custom-call(f32[24,256]{1,0:T(8,128)} %select_maximum_fusion.meta_ref, bf16[256,2560]{1,0:T(8,128)(2,1)} %copy-done.2), custom_call_target="tpu_custom_call" | custom-call | tf_op jit(solution)/shard_map/dispatch/pallas_call | solution.py:259
  69.4 68.5 %experts.1.sums_ref = f32[41120,128]{1,0:T(8,128)} custom-call(s32[128]{0:T(128)} %bitcast.13, s32[2048]{0:T(1024)} %bitcast.11, f32[2048]{0:T(1024)} %bitcast.12, bf16[1920,2560]{1,0:T(8,128)(2,1)} %get-tuple-element.12.x_ref, bf16[8,2560,1536]{2,1,0:T(8,128)(2,1)} %w1_ref.2, bf16[8,2560,1536]{2,1,0:T(8,128)(2,1)} %w3_ref.2, bf16[8,1536,2560]{2,1,0:T(8,128)(2,1)} %w2_ref.2), custom_call_target="tpu_custom_call" | custom-call | flops 36238786560 | bytes 188743680 | tf_op jit(solution)/shard_map/experts/pallas_call | solution.py:399
  137.9 0.0 copy-start.1
  138.0 96.7 %reduce_and_finish.1 = bf16[256,2560]{1,0:T(8,128)(2,1)} custom-call(f32[41120,128]{1,0:T(8,128)} %experts.1.sums_ref, bf16[256,2560]{1,0:T(8,128)(2,1)} %resid_ref.1, bf16[256,2560]{1,0:T(8,128)(2,1)} %copy-done.2, bf16[2560,3072]{1,0:T(8,128)(2,1)} %w1_ref.3, bf16[2560,3072]{1,0:T(8,128)(2,1)} %w3_ref.3, bf16[3072,2560]{1,0:T(8,128)(2,1)} %w2_ref.3), custom_call_target="tpu_custom_call" | custom-call | flops 12079595520 | bytes 47185920 | tf_op jit(solution)/shard_map/reduce_and_finish/pallas_call | solution.py:567
  234.7 2.5 %copy.15 = bf16[256,2560]{1,0:T(8,128)(2,1)} copy(bf16[256,2560]{1,0:T(8,128)(2,1)} %reduce_and_finish.1) | data formatting | bytes 2621440
  237.1 0.0 copy-done.1
  (4 shorter events, 0.1 us)
Async XLA Ops:
  0.0 4.1 %copy-start = (bf16[2560,64]{0,1:T(8,128)(2,1)S(1)}, bf16[2560,64]{0,1:T(8,128)(2,1)}, u32[]{:S(2)}) copy-start(bf16[2560,64]{0,1:T(8,128)(2,1)} %param.15) | copy-start | bytes 983044
  0.0 4.7 %copy-start.3 = (s32[256,6]{0,1:T(8,128)S(1)}, s32[256,6]{0,1:T(8,128)}, u32[]{:S(2)}) copy-start(s32[256,6]{0,1:T(8,128)} %param.12) | copy-start | bytes 18436
  4.1 1.3 copy-start.2
  137.9 99.2 %copy-start.1 = (bf16[2560,64]{0,1:T(8,128)(2,1)S(1)}, bf16[2560,64]{0,1:T(8,128)(2,1)}, u32[]{:S(2)}) copy-start(bf16[2560,64]{0,1:T(8,128)(2,1)} %param.15) | copy-start | bytes 983044

commit v2 on v1

--- a/solution.py
+++ b/solution.py
@@ -287,8 +287,8 @@
     sizes = (128, 160, 192, 224, 256)
     batch = 8
 
-    def kernel(span_ref, tok_ref, gate_ref, x_ref, w1_ref, w3_ref, w2_ref, out_ref,
-               acc, row_scr, hid, x_tile, up, down, item_e, item_base, item_count, x_sem, up_sem, down_sem, out_sem):
+    def kernel(span_ref, tok_ref, gate_ref, x_ref, w1_ref, w3_ref, w2_ref, acc,
+               row_scr, hid, x_tile, up, down, item_e, item_base, item_count, x_sem, up_sem, down_sem):
         def plan(e, n):
             count = span_ref[local_experts + e]
 
@@ -390,24 +390,21 @@
             return carry
 
         lax.fori_loop(0, n_items, item, 0)
-        out = pltpu.make_async_copy(acc, out_ref, out_sem)
-        out.start()
-        out.wait()
 
     hbm = pl.BlockSpec(memory_space=pl.ANY)
     dma = pltpu.SemaphoreType.DMA
     return pl.pallas_call(
         kernel,
-        out_shape=jax.ShapeDtypeStruct((acc_rows, LANES), F32),
+        out_shape=pltpu.VMEM((acc_rows, LANES), F32),
         grid_spec=pltpu.PrefetchScalarGridSpec(
-            num_scalar_prefetch=3, grid=(1,), in_specs=[hbm] * 4, out_specs=hbm,
+            num_scalar_prefetch=3, grid=(), in_specs=[hbm] * 4, out_specs=pl.BlockSpec(memory_space=pltpu.VMEM),
             scratch_shapes=[
-                pltpu.VMEM((acc_rows, LANES), F32), pltpu.VMEM((ROW_TILE * groups, LANES), F32),
+                pltpu.VMEM((ROW_TILE * groups, LANES), F32),
                 pltpu.VMEM((ROW_TILE, ff), BF16), pltpu.VMEM((2, ROW_TILE, width), BF16),
                 pltpu.VMEM((n_up, 2, width, up_cols), BF16), pltpu.VMEM((n_down, ff, down_cols), BF16),
                 pltpu.SMEM((max_items,), I32), pltpu.SMEM((max_items,), I32), pltpu.SMEM((max_items,), I32),
-                dma((2,)), dma((n_up, 2)), dma((n_down,)), dma]),
-        compiler_params=pltpu.CompilerParams(vmem_limit_bytes=VMEM_LIMIT),
+                dma((2,)), dma((n_up, 2)), dma((n_down,))]),
+        compiler_params=pltpu.CompilerParams(vmem_limit_bytes=34 * 1024 * 1024),
         cost_estimate=pl.CostEstimate(flops=6 * capacity * width * ff, bytes_accessed=6 * local_experts * width * ff, transcendentals=capacity * ff),
         name='experts',
     )(spans, slot_tok, slot_gate, rows_in, expert_w1, expert_w3, expert_w2)
@@ -421,15 +418,15 @@
     pieces = 4
     tok_piece = tok_local // pieces
     piece_rows = tok_piece * groups
-    up_cols = 512
+    up_cols = 256
     n_up = ff // up_cols
-    down_cols = 512
+    down_cols = 256
     n_down = width // down_cols
     add_step = 128
 
     def kernel(sums_ref, resid_ref, x_ref, w1_ref, w3_ref, w2_ref, out_ref,
-               own, pair, opp, home, up_buf, down_buf, hid, shared,
-               load_sem, pair_send, pair_recv, fwd_send, fwd_recv, bwd_send, bwd_recv, up_sem, down_sem):
+               pair, opp, home, up_buf, down_buf, hid, shared,
+               pair_send, pair_recv, fwd_send, fwd_recv, bwd_send, bwd_recv, up_sem, down_sem):
         me = lax.axis_index('ep')
         chip, core = me // 2, lax.rem(me, 2)
         sibling = 2 * chip + 1 - core
@@ -451,9 +448,6 @@
         def block_piece(b, q):
             return sums_ref.at[pl.ds((b * pieces + q) * piece_rows, piece_rows), :]
 
-        def load(o, q):
-            return pltpu.make_async_copy(block_piece(o, q), own.at[o, q], load_sem.at[o, q])
-
         def to_pair(o, q):
             return pltpu.make_async_remote_copy(
                 src_ref=block_piece(chips + o, q), dst_ref=pair.at[o, q], send_sem=pair_send.at[o, q], recv_sem=pair_recv.at[o, q],
@@ -467,7 +461,6 @@
         order = [(o, q) for o in (3, 2, 1, 0) for q in ((0, 2, 1, 3) if o == 3 else (2, 3, 0, 1) if o == 2 else (0, 1, 2, 3))]
         for o, q in order:
             to_pair(o, q).start()
-            load(o, q).start()
         for slot in range(2):
             for which in range(2):
                 up_copy(slot, slot, which).start()
@@ -475,20 +468,19 @@
         def add(o, q, src):
             def step(i, carry):
                 at = pl.ds(pl.multiple_of(i * add_step, add_step), add_step)
-                own[o, q, at, :] = own[o, q, at, :] + src[at, :]
+                pair[o, q, at, :] = pair[o, q, at, :] + src[at, :]
                 return carry
 
             lax.fori_loop(0, piece_rows // add_step, step, 0)
 
         def pair_sum(o, q):
-            load(o, q).wait()
             to_pair(o, q).wait_recv()
-            add(o, q, pair.at[o, q])
-
-        opp_fwd = [ring(own.at[3, q], opp.at[q], fwd_send, fwd_recv, q, after) for q in (0, 1)]
-        opp_bwd = [ring(own.at[3, 2 + q], opp.at[2 + q], bwd_send, bwd_recv, q, before) for q in (0, 1)]
-        home_fwd = {q: ring(own.at[2, q], home.at[0, q], fwd_send, fwd_recv, 2 + q, after) for q in range(pieces)}
-        home_bwd = {q: ring(own.at[1, q], home.at[1, q], bwd_send, bwd_recv, 2 + q, before) for q in range(pieces)}
+            add(o, q, block_piece(o, q))
+
+        opp_fwd = [ring(pair.at[3, q], opp.at[q], fwd_send, fwd_recv, q, after) for q in (0, 1)]
+        opp_bwd = [ring(pair.at[3, 2 + q], opp.at[2 + q], bwd_send, bwd_recv, q, before) for q in (0, 1)]
+        home_fwd = {q: ring(pair.at[2, q], home.at[0, q], fwd_send, fwd_recv, 2 + q, after) for q in range(pieces)}
+        home_bwd = {q: ring(pair.at[1, q], home.at[1, q], bwd_send, bwd_recv, 2 + q, before) for q in range(pieces)}
         for q in (0, 1):
             pair_sum(3, q)
             pair_sum(3, 2 + q)
@@ -553,7 +545,7 @@
             rows = slice(q * tok_piece, (q + 1) * tok_piece)
             for g in range(groups):
                 col = g * LANES
-                routed = own[0, q, pl.ds(g, tok_piece, stride=groups), :]
+                routed = pair[0, q, pl.ds(g, tok_piece, stride=groups), :]
                 total = resid_ref[rows, col:col + LANES].astype(F32) + shared[rows, col:col + LANES].astype(F32) + routed
                 out_ref[rows, col:col + LANES] = total.astype(BF16)
         for o, q in order:
@@ -567,18 +559,18 @@
     return pl.pallas_call(
         kernel,
         out_shape=jax.ShapeDtypeStruct((tok_local, width), BF16),
-        in_specs=[hbm, vmem, vmem, hbm, hbm, hbm],
+        in_specs=[vmem, vmem, vmem, hbm, hbm, hbm],
         out_specs=vmem,
         scratch_shapes=[
-            pltpu.VMEM((chips, pieces, piece_rows, LANES), F32), pltpu.VMEM((chips, pieces, piece_rows, LANES), F32),
+            pltpu.VMEM((chips, pieces, piece_rows, LANES), F32),
             pltpu.VMEM((pieces, piece_rows, LANES), F32), pltpu.VMEM((2, pieces, piece_rows, LANES), F32),
             pltpu.VMEM((2, 2, width, up_cols), BF16), pltpu.VMEM((2, ff, down_cols), BF16),
             pltpu.VMEM((tok_local, ff), BF16), pltpu.VMEM((tok_local, width), BF16),
-            dma((chips, pieces)), dma((chips, pieces)), dma((chips, pieces)), dma((6,)), dma((6,)), dma((6,)), dma((6,)), dma((2, 2)), dma((2,))],
-        compiler_params=pltpu.CompilerParams(collective_id=1, has_side_effects=True, vmem_limit_bytes=VMEM_LIMIT),
+            dma((chips, pieces)), dma((chips, pieces)), dma((6,)), dma((6,)), dma((6,)), dma((6,)), dma((2, 2)), dma((2,))],
+        compiler_params=pltpu.CompilerParams(collective_id=1, has_side_effects=True, vmem_limit_bytes=37 * 1024 * 1024),
         cost_estimate=pl.CostEstimate(flops=6 * tok_local * width * ff, bytes_accessed=6 * width * ff, transcendentals=tok_local * ff),
         name='reduce_and_finish',
-    )(sums, resid_in, normed, shared_w1, shared_w3, shared_w2)
+    )(pltpu.with_memory_space_constraint(sums, pltpu.VMEM), resid_in, normed, shared_w1, shared_w3, shared_w2)
 
 
 def solution(mesh):

time: 238 us -> 231 us (0.971)
  Pallas kernels: 229 us -> 222 us
    pallas_call x1, Pallas kernels: 68.5 us -> 63 us  [experts(): pl.pallas_call(kernel, out_shape=pltpu.VMEM((acc_rows, LANES), F32), grid...]
where the time goes in v2:
time: 231 us; the launch traced here: 230 us
  Pallas kernels  222 us (96%)
  other arithmetic  4.85 us (2%)
  local copies, waits for them, and re-layouts  2.48 us (1%)
    pallas_call x1, Pallas kernels, reduce_and_finish(): pl.pallas_call(kernel, out_shape=jax.ShapeDtypeStruct((tok_local, width),...  95.3 us
    pallas_call x1, Pallas kernels, dispatch(): pl.pallas_call(kernel, out_shape=(jax.ShapeDtypeStruct((slots, width), BF...  64 us
    pallas_call x1, Pallas kernels, experts(): pl.pallas_call(kernel, out_shape=pltpu.VMEM((acc_rows, LANES), F32), grid...  63 us

profile of v2, /device:TPU:113, one launch (start us, length us, event | category | flops | bytes accessed | tf_op | source)
XLA Modules:
  0.0 230.2 jit_solution(17661556055608877269)
XLA Ops:
  0.0 0.0 copy-start
  0.0 0.0 copy-start.3
  0.0 1.7 fusion
  1.7 0.7 convert_bitcast_fusion
  2.4 1.7 fusion.2.x_ref
  4.1 0.0 copy-done
  4.1 0.0 copy-start.2
  4.1 0.5 fusion.6
  4.7 0.0 copy-done.3
  4.8 0.1 select_reduce_fusion
  4.8 0.6 select_maximum_fusion.meta_ref
  5.5 0.0 copy-done.2
  5.5 64.0 %dispatch.1 = (bf16[1920,2560]{1,0:T(8,128)(2,1)}, s32[16,128]{1,0:T(8,128)}, f32[16,128]{1,0:T(8,128)}, s32[1,128]{1,0:T(1,128)}) custom-call(f32[24,256]{1,0:T(8,128)} %select_maximum_fusion.meta_ref, bf16[256,2560]{1,0:T(8,128)(2,1)} %copy-done.2), custom_call_target="tpu_custom_call" | custom-call | tf_op jit(solution)/shard_map/dispatch/pallas_call | solution.py:259
  69.4 63.0 %experts.1.sums_ref = f32[41120,128]{1,0:T(8,128)S(1)} custom-call(s32[128]{0:T(128)} %bitcast.13, s32[2048]{0:T(1024)} %bitcast.11, f32[2048]{0:T(1024)} %bitcast.12, bf16[1920,2560]{1,0:T(8,128)(2,1)} %get-tuple-element.12.x_ref, bf16[8,2560,1536]{2,1,0:T(8,128)(2,1)} %w1_ref.2, bf16[8,2560,1536]{2,1,0:T(8,128)(2,1)} %w3_ref.2, bf16[8,1536,2560]{2,1,0:T(8,128)(2,1)} %w2_ref.2), custom_call_target="tpu_custom_call" | custom-call | flops 36238786560 | bytes 188743680 | tf_op jit(solution)/shard_map/experts/pallas_call | solution.py:396
  132.4 0.0 copy-start.1
  132.4 95.3 %reduce_and_finish.1 = bf16[256,2560]{1,0:T(8,128)(2,1)} custom-call(f32[41120,128]{1,0:T(8,128)S(1)} %experts.1.sums_ref, bf16[256,2560]{1,0:T(8,128)(2,1)} %resid_ref.1, bf16[256,2560]{1,0:T(8,128)(2,1)} %copy-done.2, bf16[2560,3072]{1,0:T(8,128)(2,1)} %w1_ref.3, bf16[2560,3072]{1,0:T(8,128)(2,1)} %w3_ref.3, bf16[3072,2560]{1,0:T(8,128)(2,1)} %w2_ref.3), custom_call_target="tpu_custom_call" | custom-call | flops 12079595520 | bytes 47185920 | tf_op jit(solution)/shard_map/reduce_and_finish/pallas_call | solution.py:559
  227.7 2.5 %copy.15 = bf16[256,2560]{1,0:T(8,128)(2,1)} copy(bf16[256,2560]{1,0:T(8,128)(2,1)} %reduce_and_finish.1) | data formatting | bytes 2621440
  230.2 0.0 copy-done.1
  (4 shorter events, 0.1 us)
Async XLA Ops:
  0.0 4.1 %copy-start = (bf16[2560,64]{0,1:T(8,128)(2,1)S(1)}, bf16[2560,64]{0,1:T(8,128)(2,1)}, u32[]{:S(2)}) copy-start(bf16[2560,64]{0,1:T(8,128)(2,1)} %param.15) | copy-start | bytes 983044
  0.0 4.7 %copy-start.3 = (s32[256,6]{0,1:T(8,128)S(1)}, s32[256,6]{0,1:T(8,128)}, u32[]{:S(2)}) copy-start(s32[256,6]{0,1:T(8,128)} %param.12) | copy-start | bytes 18436
  4.1 1.3 copy-start.2
  132.4 97.8 %copy-start.1 = (bf16[2560,64]{0,1:T(8,128)(2,1)S(1)}, bf16[2560,64]{0,1:T(8,128)(2,1)}, u32[]{:S(2)}) copy-start(bf16[2560,64]{0,1:T(8,128)(2,1)} %param.15) | copy-start | bytes 983044

commit v3 on v2

--- a/solution.py
+++ b/solution.py
@@ -11,20 +11,43 @@
 LANES = 128
 ROW_TILE = 256
 ALIGN = 16
-VMEM_LIMIT = 60 * 1024 * 1024
 F32, BF16, I32 = jnp.float32, jnp.bfloat16, jnp.int32
 
 
-def rms_norm(resid_in, norm_gain):
-    resid32 = resid_in.astype(F32)
-    inv_rms = lax.rsqrt(jnp.mean(resid32 * resid32, axis=1, keepdims=True) + NORM_EPS)
-    return (resid32 * inv_rms * norm_gain).astype(BF16)
-
-
-def gate_values(normed, router_w, expert_ids):
-    probs = jax.nn.softmax(jnp.dot(normed, router_w, preferred_element_type=F32), axis=1)
-    hit = expert_ids[:, :, None] == jnp.arange(probs.shape[1], dtype=I32)
-    return ROUTE_SCALE * jnp.sum(jnp.where(hit, probs[:, None, :], 0.0), axis=2)
+def norm_and_gates(resid_in, norm_gain, router_t, ids_t, prio_t):
+    tok_local, width = resid_in.shape
+    top_k = ids_t.shape[0]
+    n_experts = router_t.shape[0]
+
+    def kernel(resid_ref, gain_ref, router_ref, ids_ref, prio_ref, x_ref, meta_ref):
+        resid32 = resid_ref[...].astype(F32)
+        inv_rms = lax.rsqrt(jnp.mean(resid32 * resid32, axis=1, keepdims=True) + NORM_EPS)
+        normed = (resid32 * inv_rms * gain_ref[...]).astype(BF16)
+        x_ref[...] = normed
+        logits = lax.dot_general(normed, router_ref[...], (((1,), (1,)), ((), ())), preferred_element_type=F32)
+        powers = jnp.exp(logits - jnp.max(logits, axis=1, keepdims=True))
+        probs = powers / jnp.sum(powers, axis=1, keepdims=True)
+        meta_ref[0:8, :] = jnp.full((8, tok_local), -1.0e6, F32)
+        meta_ref[8:, :] = jnp.zeros((16, tok_local), F32)
+        meta_ref[0:top_k, :] = ids_ref[...].astype(F32)
+        meta_ref[8:8 + top_k, :] = prio_ref[...].astype(F32)
+        eye = lax.broadcasted_iota(I32, (LANES, LANES), 0) == lax.broadcasted_iota(I32, (LANES, LANES), 1)
+        expert = lax.broadcasted_iota(I32, (LANES, n_experts), 1).astype(F32)
+        for h in range(tok_local // LANES):
+            span = slice(h * LANES, (h + 1) * LANES)
+            for k in range(top_k):
+                id_col = jnp.sum(jnp.where(eye, ids_ref[k:k + 1, span].astype(F32), 0.0), axis=1, keepdims=True)
+                gate_col = ROUTE_SCALE * jnp.sum(jnp.where(expert == id_col, probs[span, :], 0.0), axis=1, keepdims=True)
+                meta_ref[16 + k:17 + k, span] = jnp.sum(jnp.where(eye, gate_col, 0.0), axis=0, keepdims=True)
+
+    vmem = pl.BlockSpec(memory_space=pltpu.VMEM)
+    return pl.pallas_call(
+        kernel,
+        out_shape=(jax.ShapeDtypeStruct((tok_local, width), BF16), jax.ShapeDtypeStruct((24, tok_local), F32)),
+        in_specs=[vmem] * 5, out_specs=(vmem, vmem),
+        compiler_params=pltpu.CompilerParams(vmem_limit_bytes=30 * 1024 * 1024),
+        name='norm_and_gates',
+    )(resid_in, norm_gain.reshape(1, width), router_t, ids_t, prio_t)
 
 
 def dispatch(meta, normed, local_experts, capacity, slots, ep_size):
@@ -40,7 +63,7 @@
     n_rows = tok_tiles * 8
     used = capacity + local_experts * ALIGN
     slot_tiles = used // LANES
-    sel_step = used // 4
+    sel_step = used // 2
     moves = [(dc, ds) for ds in range(2) for dc in range(chips) if (dc, ds) != (0, 0)]
     seen_from = {0: 0, 1: 1, chips - 1: 2, 2: 3}
 
@@ -259,18 +282,18 @@
     return pl.pallas_call(
         kernel,
         out_shape=(
-            jax.ShapeDtypeStruct((slots, width), BF16),
+            pltpu.HBM((slots, width), BF16),
             jax.ShapeDtypeStruct((table_rows, LANES), I32),
             jax.ShapeDtypeStruct((table_rows, LANES), F32),
             jax.ShapeDtypeStruct((1, LANES), I32)),
         in_specs=[vmem, vmem],
-        out_specs=(pl.BlockSpec(memory_space=pl.ANY), vmem, vmem, vmem),
+        out_specs=(pl.BlockSpec(memory_space=pltpu.HBM), vmem, vmem, vmem),
         scratch_shapes=[
             pltpu.VMEM((ep_size, meta_rows, tok_local), F32), pltpu.VMEM((chunks, n_tokens, piece), BF16),
             pltpu.VMEM((used, n_tokens), BF16), pltpu.VMEM((2, used, piece), BF16),
             pltpu.VMEM((n_rows, LANES), F32), pltpu.VMEM((local_experts, n_tokens), F32), pltpu.VMEM((used, 32), F32),
             dma((len(moves),)), dma((len(moves),)), dma((9, chunks)), dma((9, chunks)), dma((2,))],
-        compiler_params=pltpu.CompilerParams(collective_id=0, has_side_effects=True, vmem_limit_bytes=VMEM_LIMIT),
+        compiler_params=pltpu.CompilerParams(collective_id=0, has_side_effects=True, vmem_limit_bytes=36 * 1024 * 1024),
         name='dispatch',
     )(meta, normed)
 
@@ -537,15 +560,19 @@
             opp_bwd[q].wait_recv()
             add(1, 2 + q, opp.at[2 + q])
             home_bwd[2 + q].start()
+        for q in (0, 1):
+            home_fwd[2 + q].wait_recv()
+            add(0, 2 + q, home.at[0, 2 + q])
+            home_bwd[q].wait_recv()
+            add(0, q, home.at[1, q])
         for q in (0, 2, 1, 3):
-            home_fwd[q].wait_recv()
-            home_bwd[q].wait_recv()
-            add(0, q, home.at[0, q])
-            add(0, q, home.at[1, q])
+            way, late = (0, home_fwd[q]) if q < 2 else (1, home_bwd[q])
+            late.wait_recv()
             rows = slice(q * tok_piece, (q + 1) * tok_piece)
             for g in range(groups):
                 col = g * LANES
-                routed = pair[0, q, pl.ds(g, tok_piece, stride=groups), :]
+                at = pl.ds(g, tok_piece, stride=groups)
+                routed = pair[0, q, at, :] + home[way, q, at, :]
                 total = resid_ref[rows, col:col + LANES].astype(F32) + shared[rows, col:col + LANES].astype(F32) + routed
                 out_ref[rows, col:col + LANES] = total.astype(BF16)
         for o, q in order:
@@ -558,7 +585,7 @@
     dma = pltpu.SemaphoreType.DMA
     return pl.pallas_call(
         kernel,
-        out_shape=jax.ShapeDtypeStruct((tok_local, width), BF16),
+        out_shape=pltpu.VMEM((tok_local, width), BF16),
         in_specs=[vmem, vmem, vmem, hbm, hbm, hbm],
         out_specs=vmem,
         scratch_shapes=[
@@ -585,13 +612,7 @@
         capacity = tok_local * top_k
         n_tokens = tok_local * ep_size
         slots = -(-(capacity + local_experts * ALIGN + ROW_TILE) // LANES) * LANES
-        normed = rms_norm(resid_in, norm_gain)
-        gates = gate_values(normed, router_w, expert_ids)
-
-        def rows8(x, fill):
-            return jnp.pad(x.astype(F32).T, ((0, 8 - top_k), (0, 0)), constant_values=fill)
-
-        meta = jnp.concatenate([rows8(expert_ids, -1.0e6), rows8(priority, 0.0), rows8(gates, 0.0)], axis=0)
+        normed, meta = norm_and_gates(resid_in, norm_gain, router_w.T, expert_ids.T, priority.T)
         rows_in, slot_tok, slot_gate, spans = dispatch(meta, normed, local_experts, capacity, slots, ep_size)
         spans = spans.reshape(-1)
         sums = experts(spans, slot_tok.reshape(-1), slot_gate.reshape(-1), rows_in, expert_w1, expert_w3, expert_w2, n_tokens, capacity)

time: 231 us -> 226 us (0.978)
  other arithmetic: 4.85 us -> 0 us
  local copies, waits for them, and re-layouts: 2.48 us -> 6.63 us
  Pallas kernels: 222 us -> 219 us
    unnamed x9 -> x17, local copies, waits for them, and re-layouts: 2.48 us -> 5.92 us
    pallas_call x2 -> x3, Pallas kernels: 159 us -> 156 us  [the longest x1 93.7 us: reduce_and_finish(): pl.pallas_call(kernel, out_shape=pltpu.VMEM((tok_local, width), BF16), in...]
where the time goes in v3:
time: 226 us; the launch traced here: 225 us
  Pallas kernels  219 us (97%)
  local copies, waits for them, and re-layouts  6.63 us (3%)
    pallas_call x1, Pallas kernels, reduce_and_finish(): pl.pallas_call(kernel, out_shape=pltpu.VMEM((tok_local, width), BF16), in...  93.7 us
    pallas_call x1, Pallas kernels, experts(): pl.pallas_call(kernel, out_shape=pltpu.VMEM((acc_rows, LANES), F32), grid...  62.6 us
    pallas_call x1, Pallas kernels, dispatch(): pl.pallas_call(kernel, out_shape=(pltpu.HBM((slots, width), BF16), jax.Sh...  61.2 us
    unnamed x17, local copies, waits for them, and re-layouts  5.92 us

profile of v3, /device:TPU:113, one launch (start us, length us, event | category | flops | bytes accessed | tf_op | source)
XLA Modules:
  0.0 225.4 jit_solution(12696825894130485899)
XLA Ops:
  0.0 0.7 reshape.12.gain_ref
  0.7 0.0 copy-start
  0.7 1.3 copy-done
  2.0 0.0 copy-start.2
  2.0 1.0 copy-done.2
  3.0 0.0 copy-start.3
  3.0 0.7 copy-done.3
  3.7 0.0 copy-start.4
  3.7 0.7 copy-done.4
  4.4 1.2 norm_and_gates.1
  5.6 0.0 copy-start.1
  5.7 61.2 %dispatch.1 = (bf16[1920,2560]{1,0:T(8,128)(2,1)}, s32[16,128]{1,0:T(8,128)S(1)}, f32[16,128]{1,0:T(8,128)S(1)}, s32[1,128]{1,0:T(1,128)S(1)}) custom-call(f32[24,256]{1,0:T(8,128)S(1)} %get-tuple-element.11.meta_ref, bf16[256,2560]{1,0:T(8,128)(2,1)S(1)} %get-tuple-element.12.x_ref), custom_call_target="tpu_custom_call" | custom-call | tf_op jit(solution)/shard_map/dispatch/pallas_call | solution.py:282
  66.9 0.0 copy-start.6
  66.9 0.6 copy-done.6
  67.5 0.0 copy-start.5
  67.5 0.0 copy-start.7
  67.5 0.6 copy-done.5
  68.1 0.0 copy-done.7
  68.1 62.6 %experts.1.sums_ref = f32[41120,128]{1,0:T(8,128)S(1)} custom-call(s32[128]{0:T(128)} %bitcast.11, s32[2048]{0:T(1024)} %bitcast.9, f32[2048]{0:T(1024)} %bitcast.10, bf16[1920,2560]{1,0:T(8,128)(2,1)} %get-tuple-element.16.x_ref, bf16[8,2560,1536]{2,1,0:T(8,128)(2,1)} %w1_ref.2, bf16[8,2560,1536]{2,1,0:T(8,128)(2,1)} %w3_ref.2, bf16[8,1536,2560]{2,1,0:T(8,128)(2,1)} %w2_ref.2), custom_call_target="tpu_custom_call" | custom-call | flops 36238786560 | bytes 188743680 | tf_op jit(solution)/shard_map/experts/pallas_call | solution.py:419
  130.7 0.0 copy-done.1
  130.7 93.7 %reduce_and_finish.1 = bf16[256,2560]{1,0:T(8,128)(2,1)S(1)} custom-call(f32[41120,128]{1,0:T(8,128)S(1)} %experts.1.sums_ref, bf16[256,2560]{1,0:T(8,128)(2,1)} %resid_ref.3, bf16[256,2560]{1,0:T(8,128)(2,1)} %copy-done.1, bf16[2560,3072]{1,0:T(8,128)(2,1)} %w1_ref.3, bf16[2560,3072]{1,0:T(8,128)(2,1)} %w3_ref.3, bf16[3072,2560]{1,0:T(8,128)(2,1)} %w2_ref.3), custom_call_target="tpu_custom_call" | custom-call | flops 12079595520 | bytes 47185920 | tf_op jit(solution)/shard_map/reduce_and_finish/pallas_call | solution.py:586
  224.4 1.1 copy.13
Async XLA Ops:
  0.7 1.3 copy-start
  2.0 1.0 copy-start.2
  3.0 0.7 copy-start.3
  3.7 0.7 copy-start.4
  5.6 125.0 %copy-start.1 = (bf16[256,2560]{1,0:T(8,128)(2,1)}, bf16[256,2560]{1,0:T(8,128)(2,1)S(1)}, u32[]{:S(2)}) copy-start(bf16[256,2560]{1,0:T(8,128)(2,1)S(1)} %get-tuple-element.12.x_ref) | copy-start | bytes 3932164
  66.9 0.6 copy-start.6
  67.5 0.6 copy-start.5
  67.5 0.6 copy-start.7

commit v4 on v3

--- a/solution.py
+++ b/solution.py
@@ -19,7 +19,13 @@
     top_k = ids_t.shape[0]
     n_experts = router_t.shape[0]
 
-    def kernel(resid_ref, gain_ref, router_ref, ids_ref, prio_ref, x_ref, meta_ref):
+    def kernel(resid_hbm, gain_hbm, router_hbm, ids_hbm, prio_hbm, x_ref, meta_ref, resid_ref, gain_ref, router_ref, ids_ref, prio_ref, sem):
+        pairs = ((resid_hbm, resid_ref), (gain_hbm, gain_ref), (router_hbm, router_ref), (ids_hbm, ids_ref), (prio_hbm, prio_ref))
+        copies = [pltpu.make_async_copy(src, dst, sem.at[i]) for i, (src, dst) in enumerate(pairs)]
+        for copy in copies:
+            copy.start()
+        for copy in copies:
+            copy.wait()
         resid32 = resid_ref[...].astype(F32)
         inv_rms = lax.rsqrt(jnp.mean(resid32 * resid32, axis=1, keepdims=True) + NORM_EPS)
         normed = (resid32 * inv_rms * gain_ref[...]).astype(BF16)
@@ -44,10 +50,12 @@
     return pl.pallas_call(
         kernel,
         out_shape=(jax.ShapeDtypeStruct((tok_local, width), BF16), jax.ShapeDtypeStruct((24, tok_local), F32)),
-        in_specs=[vmem] * 5, out_specs=(vmem, vmem),
+        in_specs=[pl.BlockSpec(memory_space=pltpu.HBM)] * 5, out_specs=(vmem, vmem),
+        scratch_shapes=[pltpu.VMEM(resid_in.shape, BF16), pltpu.VMEM((1, width), F32), pltpu.VMEM(router_t.shape, BF16),
+                        pltpu.VMEM(ids_t.shape, I32), pltpu.VMEM(prio_t.shape, I32), pltpu.SemaphoreType.DMA((5,))],
         compiler_params=pltpu.CompilerParams(vmem_limit_bytes=30 * 1024 * 1024),
         name='norm_and_gates',
-    )(resid_in, norm_gain.reshape(1, width), router_t, ids_t, prio_t)
+    )(*[pltpu.with_memory_space_constraint(x, pltpu.HBM) for x in (resid_in, norm_gain.reshape(1, width), router_t, ids_t, prio_t)])
 
 
 def dispatch(meta, normed, local_experts, capacity, slots, ep_size):

time: 226 us -> 224 us (level)
  local copies, waits for them, and re-layouts: 6.63 us -> 3.56 us
    unnamed x17 -> x9, local copies, waits for them, and re-layouts: 5.92 us -> 2.24 us
where the time goes in v4:
time: 224 us; the launch traced here: 225 us
  Pallas kernels  221 us (99%)
  local copies, waits for them, and re-layouts  3.56 us (2%)
    pallas_call x1, Pallas kernels, reduce_and_finish(): pl.pallas_call(kernel, out_shape=pltpu.VMEM((tok_local, width), BF16), in...  95.8 us
    pallas_call x1, Pallas kernels, experts(): pl.pallas_call(kernel, out_shape=pltpu.VMEM((acc_rows, LANES), F32), grid...  61.3 us
    pallas_call x1, Pallas kernels, dispatch(): pl.pallas_call(kernel, out_shape=(pltpu.HBM((slots, width), BF16), jax.Sh...  61.3 us

profile of v4, /device:TPU:113, one launch (start us, length us, event | category | flops | bytes accessed | tf_op | source)
XLA Modules:
  0.0 224.6 jit_solution(17412768180525144205)
XLA Ops:
  0.0 1.3 reshape.12.gain_hbm
  1.3 2.6 %norm_and_gates.1 = (bf16[256,2560]{1,0:T(8,128)(2,1)S(1)}, f32[24,256]{1,0:T(8,128)S(1)}) custom-call(bf16[256,2560]{1,0:T(8,128)(2,1)} %resid_ref.1, f32[1,2560]{1,0:T(1,128)} %reshape.12.gain_hbm, bf16[64,2560]{1,0:T(8,128)(2,1)} %bitcast.9, s32[6,256]{1,0:T(8,128)} %bitcast.10, s32[6,256]{1,0:T(8,128)} %bitcast.11), custom_call_target="tpu_custom_call" | custom-call | tf_op jit(solution)/shard_map/norm_and_gates/pallas_call | solution.py:50
  4.0 0.0 copy-start
  4.0 61.3 %dispatch.1 = (bf16[1920,2560]{1,0:T(8,128)(2,1)}, s32[16,128]{1,0:T(8,128)S(1)}, f32[16,128]{1,0:T(8,128)S(1)}, s32[1,128]{1,0:T(1,128)S(1)}) custom-call(f32[24,256]{1,0:T(8,128)S(1)} %get-tuple-element.11.meta_ref, bf16[256,2560]{1,0:T(8,128)(2,1)S(1)} %get-tuple-element.12.x_ref), custom_call_target="tpu_custom_call" | custom-call | tf_op jit(solution)/shard_map/dispatch/pallas_call | solution.py:290
  65.3 0.0 copy-start.2
  65.3 0.6 copy-done.2
  65.9 0.0 copy-start.1
  65.9 0.0 copy-start.3
  65.9 0.6 copy-done.1
  66.5 0.0 copy-done.3
  66.5 61.3 %experts.1.sums_ref = f32[41120,128]{1,0:T(8,128)S(1)} custom-call(s32[128]{0:T(128)} %bitcast.8, s32[2048]{0:T(1024)} %bitcast.6, f32[2048]{0:T(1024)} %bitcast.7, bf16[1920,2560]{1,0:T(8,128)(2,1)} %get-tuple-element.16.x_ref, bf16[8,2560,1536]{2,1,0:T(8,128)(2,1)} %w1_ref.2, bf16[8,2560,1536]{2,1,0:T(8,128)(2,1)} %w3_ref.2, bf16[8,1536,2560]{2,1,0:T(8,128)(2,1)} %w2_ref.2), custom_call_target="tpu_custom_call" | custom-call | flops 36238786560 | bytes 188743680 | tf_op jit(solution)/shard_map/experts/pallas_call | solution.py:427
  127.8 0.0 copy-done
  127.8 95.8 %reduce_and_finish.1 = bf16[256,2560]{1,0:T(8,128)(2,1)S(1)} custom-call(f32[41120,128]{1,0:T(8,128)S(1)} %experts.1.sums_ref, bf16[256,2560]{1,0:T(8,128)(2,1)} %resid_ref.1, bf16[256,2560]{1,0:T(8,128)(2,1)} %copy-done, bf16[2560,3072]{1,0:T(8,128)(2,1)} %w1_ref.3, bf16[2560,3072]{1,0:T(8,128)(2,1)} %w3_ref.3, bf16[3072,2560]{1,0:T(8,128)(2,1)} %w2_ref.3), custom_call_target="tpu_custom_call" | custom-call | flops 12079595520 | bytes 47185920 | tf_op jit(solution)/shard_map/reduce_and_finish/pallas_call | solution.py:594
  223.6 1.1 copy.13
Async XLA Ops:
  4.0 123.8 %copy-start = (bf16[256,2560]{1,0:T(8,128)(2,1)}, bf16[256,2560]{1,0:T(8,128)(2,1)S(1)}, u32[]{:S(2)}) copy-start(bf16[256,2560]{1,0:T(8,128)(2,1)S(1)} %get-tuple-element.12.x_ref) | copy-start | bytes 3932164
  65.3 0.6 copy-start.2
  65.9 0.6 copy-start.1
  65.9 0.6 copy-start.3
